TPU v7x, 32 devices: a whole 2x2x4 slice. The times are simulated.
32 devices in a mesh: sector: 8 (over z, y), ops: 4 (over x, core).
Axes of the slice: x: 2, y: 2, z: 4, core: 2. Of those that a mesh axis runs over, the one named last changes fastest.
Arguments:
- wavefunction: float32 [8, 640, 640], P('sector'), may hold values from -160 to 160
- left_env: float32 [8, 16, 640, 640], P('sector', 'ops'), may hold values from -0.25 to 0.25
- right_env: float32 [8, 16, 640, 640], P('sector', 'ops'), may hold values from -0.25 to 0.25
- shift_map: int32 [4, 8], P('ops'), may hold values from 0 to 7, each once within a row
- op_counts: int32 [4, 8], P('ops', 'sector'), may hold values from 1 to 4
Outputs:
- updated_tensor: float32 [8, 640, 640], P('sector', None, 'ops')
- rotated_env: float32 [8, 16, 640, 640], P('sector', 'ops')
Inputs may be any that keep to these rules, and one draw needn't show every extreme that they name: `shift_map`: each row lists every sector once.
All inputs are finite; a program needn't handle non-finite values.
Results may differ from a plain program's by a relative error of at most 0.0003.
Values sent between devices are 32-bit elements; how exact they have to be, the bound alone decides.
A program may use at most 128 MiB of HBM per device.

v0:
```python
import functools
import math

import jax
import jax.numpy as jnp
from jax import lax
from jax.experimental import pallas as pl
from jax.experimental.pallas import tpu as pltpu
from jax.sharding import PartitionSpec as P

POLAR = 5
LANES, SUBLANES = 128, 8
CORES = 2
AHEAD = 3
MESH = pl.DeviceIdType.MESH
F32, BF16 = jnp.float32, jnp.bfloat16

precise = lax.Precision.HIGH


def dot(a, b):
    return jnp.dot(a, b, precision=precise, preferred_element_type=jnp.float32)


def to_tiles(block, padded):
    rows, cols = block.shape
    tiles = block.reshape(rows // SUBLANES, SUBLANES, cols // LANES, LANES)
    tiles = tiles.transpose(0, 2, 1, 3).reshape(rows * cols // (SUBLANES * LANES), SUBLANES, LANES)
    return jnp.pad(tiles, ((0, padded - tiles.shape[0]), (0, 0), (0, 0)))


def from_tiles(tiles, rows, cols):
    tiles = tiles[: rows * cols // (SUBLANES * LANES)]
    tiles = tiles.reshape(rows // SUBLANES, cols // LANES, SUBLANES, LANES)
    return tiles.transpose(0, 2, 1, 3).reshape(rows, cols)


def swap(value, axis, bit):
    size = lax.axis_size(axis)
    return lax.ppermute(value, axis, [(i, i ^ bit) for i in range(size)])


def sum_scatter(tiles, axis):
    size, here = lax.axis_size(axis), lax.axis_index(axis)
    rest = tiles.reshape((size, tiles.shape[0] // size) + tiles.shape[1:])
    bit = 1
    while bit < size:
        mine = (here // bit) % 2
        pairs = rest.reshape((rest.shape[0] // 2, 2) + rest.shape[1:])
        keep = lax.dynamic_index_in_dim(pairs, mine, 1, keepdims=False)
        give = lax.dynamic_index_in_dim(pairs, 1 - mine, 1, keepdims=False)
        rest = keep + swap(give, axis, bit)
        bit *= 2
    return rest[0]


def gather_whole(quarter, axis):
    size, here = lax.axis_size(axis), lax.axis_index(axis)
    held = quarter[None]
    bit = size // 2
    while bit:
        mine = (here // bit) % 2
        other = swap(held, axis, bit)
        first = jnp.where(mine == 0, held, other)
        second = jnp.where(mine == 0, other, held)
        held = jnp.stack([first, second], axis=1).reshape((-1,) + quarter.shape)
        bit //= 2
    return held.reshape((-1,) + quarter.shape[1:])


def polar(sigma_block):
    states = sigma_block.shape[0]
    mean_sq = jnp.sum(sigma_block * sigma_block) / float(states * states)
    iterate = sigma_block * (lax.rsqrt(states * mean_sq + 1e-06) / 2.2)

    def step(_, iterate):
        gram_matrix = jnp.einsum("ab,cb->ac", iterate, iterate, precision=precise)
        return 1.5 * iterate - 0.5 * dot(gram_matrix, iterate)

    return lax.fori_loop(0, POLAR, step, iterate) * math.sqrt(states)


def shards_general(wavefunction, left_env, right_env, shift_map, op_counts):
    sector_count = lax.axis_size("sector")
    group_size = lax.axis_size("ops")
    group_here = lax.axis_index("ops")
    states = wavefunction.shape[1]
    ops_here = left_env.shape[1]
    parts = sector_count * group_size
    piece = -(-states * states // (SUBLANES * LANES * parts))
    padded = piece * parts
    quarter = piece * sector_count

    whole_map = lax.all_gather(shift_map[0], "ops").reshape(parts)

    def fetch_from_quarter(own_quarter):
        pieces = own_quarter.reshape(sector_count, piece, SUBLANES, LANES)
        spread = lax.all_to_all(pieces, "sector", split_axis=0, concat_axis=0, tiled=True)
        picked = jnp.take(spread, whole_map, axis=0)
        landed = lax.all_to_all(picked, ("ops", "sector"), split_axis=0, concat_axis=0, tiled=True)
        return from_tiles(landed.reshape(padded, SUBLANES, LANES), states, states)

    psi_tiles = to_tiles(wavefunction[0], padded)
    psi_quarter = lax.dynamic_slice_in_dim(psi_tiles, group_here * quarter, quarter, 0)
    moved_block = fetch_from_quarter(psi_quarter)

    left, right = left_env[0], right_env[0]
    count = op_counts[0, 0]
    active = (jnp.arange(ops_here) < count).astype(jnp.float32)
    left_psi = jnp.einsum("wab,bc->wac", left, moved_block, precision=precise) * active[:, None, None]
    partial_sigma = jnp.einsum("wac,wcd->ad", left_psi, right, precision=precise)

    sigma_quarter = sum_scatter(to_tiles(partial_sigma, padded), "ops")
    source_sigma = fetch_from_quarter(sigma_quarter)
    sigma_block = from_tiles(gather_whole(sigma_quarter, "ops"), states, states)

    whole_tensor = polar(sigma_block)
    column_width = states // group_size
    own_columns = lax.dynamic_slice_in_dim(whole_tensor, group_here * column_width, column_width, 1)
    half_rotated = jnp.einsum("ba,wbc->wac", whole_tensor, left, precision=precise)
    source_tensor = polar(source_sigma)
    rotated = jnp.einsum("wac,cd->wad", half_rotated, source_tensor, precision=precise)
    return (own_columns[None], rotated[None])


def halves(value):
    high = value.astype(BF16)
    return high, (value - high.astype(F32)).astype(BF16)


def bdot(a, b):
    return jnp.dot(a, b, preferred_element_type=F32)


class Place:
    def __init__(self, nsec, nops, ny, states):
        self.nsec, self.nops, self.ny, self.nz = nsec, nops, ny, nsec // ny
        self.states = states
        self.chunks = states // LANES
        self.parts = nops * ny
        self.rows = states // self.parts
        self.quarter = states // nops
        self.dests = nops * ny

    def locate(self):
        self.s, self.o = lax.axis_index("sector"), lax.axis_index("ops")
        self.z, self.y = self.s // self.ny, lax.rem(self.s, self.ny)
        self.part = self.o * self.ny + self.y

    def plane_peer(self, index, sign=1):
        dy, do = index // self.nops, index % self.nops
        if sign < 0:
            dy, do = (self.ny - dy) % self.ny, (self.nops - do) % self.nops
        return lax.rem(self.y + dy, self.ny), lax.rem(self.o + do, self.nops)

    def greet(self):
        barrier = pltpu.get_barrier_semaphore()
        for index in range(1, self.dests):
            y, o = self.plane_peer(index)
            pl.semaphore_signal(barrier, inc=1, device_id=(self.z * self.ny + y, o), device_id_type=MESH)

        @pl.when(self.z > 0)
        def _():
            pl.semaphore_signal(barrier, inc=1, device_id=(self.s - self.ny, self.o), device_id_type=MESH)

        @pl.when(self.z < self.nz - 1)
        def _():
            pl.semaphore_signal(barrier, inc=1, device_id=(self.s + self.ny, self.o), device_id_type=MESH)

        line = (self.z > 0).astype(jnp.int32) + (self.z < self.nz - 1).astype(jnp.int32)
        pl.semaphore_wait(barrier, self.dests - 1 + line)


class Maps:
    def __init__(self, place, own_ref, rows_ref, scalars_ref, sems):
        self.place, self.own, self.rows, self.scalars, self.sems = place, own_ref, rows_ref, scalars_ref, sems

    @staticmethod
    def scratch(place):
        return [
            pltpu.VMEM((place.nops, 1, LANES), jnp.int32),
            pltpu.SMEM((place.nops, 1, LANES), jnp.int32),
            pltpu.SemaphoreType.DMA((3, place.nops)),
        ]

    def copy(self, offset, sign):
        p = self.place
        peer = lax.rem(p.o + offset, p.nops)
        slot = p.o if sign > 0 else lax.rem(p.o + p.nops - offset, p.nops)
        return pltpu.make_async_remote_copy(
            self.own, self.rows.at[slot], self.sems.at[0, offset], self.sems.at[1, offset],
            device_id=(p.s, peer), device_id_type=MESH)

    def start(self):
        for offset in range(1, self.place.nops):
            self.copy(offset, 1).start()
        pltpu.make_async_copy(self.own, self.rows.at[self.place.o], self.sems.at[2, 0]).start()

    def finish(self):
        for offset in range(1, self.place.nops):
            self.copy(offset, 1).wait_send()
            self.copy(offset, -1).wait_recv()
        pltpu.make_async_copy(self.own, self.rows.at[self.place.o], self.sems.at[2, 0]).wait()
        landed = pltpu.make_async_copy(self.rows, self.scalars, self.sems.at[2, 1])
        landed.start()
        landed.wait()

    def want(self, y, o):
        return self.scalars[o, 0, self.place.z * self.place.ny + y]


class Fetch:
    def __init__(self, place, maps, piece, held, stage, landed, up, down, across, within, local):
        self.place, self.maps, self.piece = place, maps, piece
        self.held, self.stage, self.landed = held, stage, landed
        self.up, self.down, self.across, self.within, self.local = up, down, across, within, local

    @staticmethod
    def scratch(place):
        c, dma = place.chunks, pltpu.SemaphoreType.DMA
        return (
            [pltpu.VMEM((place.nsec, place.rows, LANES), F32) for _ in range(c)],
            pltpu.VMEM((c, place.dests, place.rows, LANES), F32),
            dma((2, c, place.nz - 1)),
            dma((2, c, place.nz - 1)),
            dma((2, c, place.ny)),
            dma((2, c, place.dests)),
            dma((c,)),
        )

    def across_copy(self, j, dy, sign):
        p = self.place
        y = lax.rem(p.y + dy, p.ny)
        slot = p.s if sign > 0 else p.z * p.ny + lax.rem(p.y + p.ny - dy, p.ny)
        return pltpu.make_async_remote_copy(
            self.piece(j, y), self.held[j].at[slot], self.across.at[0, j, dy], self.across.at[1, j, dy],
            device_id=(p.z * p.ny + y, p.o), device_id_type=MESH)

    def own_copy(self, j):
        p = self.place
        return pltpu.make_async_copy(self.piece(j, p.y), self.held[j].at[p.s], self.local.at[j])

    def begin(self, j):
        for dy in range(1, self.place.ny):
            self.across_copy(j, dy, 1).start()
        self.own_copy(j).start()

    def line_copy(self, j, k, direction):
        p = self.place
        slab = self.held[j].at[pl.ds((p.z - direction * k) * p.ny, p.ny)]
        sems = self.up if direction > 0 else self.down
        return pltpu.make_async_remote_copy(
            slab, slab, sems.at[0, j, k], sems.at[1, j, k],
            device_id=(p.s + direction * p.ny, p.o), device_id_type=MESH)

    def line_wait(self, j, k, direction):
        p = self.place
        slab = self.held[j].at[pl.ds((p.z - direction * k) * p.ny, p.ny)]
        sems = self.up if direction > 0 else self.down
        pltpu.make_async_remote_copy(
            slab, slab, sems.at[0, j, k - 1], sems.at[1, j, k - 1],
            device_id=(p.s - direction * p.ny, p.o), device_id_type=MESH).wait_recv()

    def has(self, k, direction):
        return self.place.z >= k if direction > 0 else self.place.z < self.place.nz - k

    def more(self, direction):
        return self.place.z < self.place.nz - 1 if direction > 0 else self.place.z > 0

    def send_own(self, j):
        for dy in range(1, self.place.ny):
            self.across_copy(j, dy, -1).wait_recv()
        self.own_copy(j).wait()
        for direction in (1, -1):
            @pl.when(self.more(direction))
            def _():
                self.line_copy(j, 0, direction).start()

    def forward(self, j, k):
        for direction in (1, -1):
            @pl.when(self.has(k, direction))
            def _():
                self.line_wait(j, k, direction)

            if k < self.place.nz - 1:
                @pl.when(self.has(k, direction) & self.more(direction))
                def _():
                    self.line_copy(j, k, direction).start()

    def within_copy(self, j, index, sign):
        p = self.place
        y, o = p.plane_peer(index, sign)
        part = p.part if sign > 0 else o * p.ny + y
        return pltpu.make_async_remote_copy(
            self.stage.at[j, index], self.landed.at[j, pl.ds(part * p.rows, p.rows)],
            self.within.at[0, j, index], self.within.at[1, j, index],
            device_id=(p.z * p.ny + y, o), device_id_type=MESH)

    def hand_out(self, j):
        p = self.place
        order = sorted(range(p.dests), key=lambda index: -((index // p.nops > 0) + (index % p.nops > 0)))
        for index in order:
            y, o = p.plane_peer(index)
            picked = self.held[j][self.maps.want(y, o)]
            if index == 0:
                self.landed[j, pl.ds(p.part * p.rows, p.rows)] = picked
            else:
                self.stage[j, index] = picked
                self.within_copy(j, index, 1).start()

    def receive(self, j):
        for index in range(1, self.place.dests):
            self.within_copy(j, index, -1).wait_recv()

    def drain(self):
        for j in range(self.place.chunks):
            for dy in range(1, self.place.ny):
                self.across_copy(j, dy, 1).wait_send()
            for direction in (1, -1):
                for k in range(self.place.nz - 1):
                    @pl.when(self.has(k, direction) & self.more(direction))
                    def _():
                        self.line_copy(j, k, direction).wait_send()
            for index in range(1, self.place.dests):
                self.within_copy(j, index, 1).wait_send()


def tdot(a, b):
    return lax.dot_general(a, b, (((1,), (1,)), ((), ())), preferred_element_type=F32)


class Polar:
    def __init__(self, n, block, cols, rows, gram):
        self.n, self.block, self.cols, self.rows, self.gram = n, block, cols, rows, gram

    @staticmethod
    def scratch(n):
        return [pltpu.VMEM((n, 2 * n), BF16), pltpu.VMEM((2 * n, n), BF16), pltpu.VMEM((2 * n, n), BF16)]

    def normalise(self, sigma):
        n = self.n
        squares = jnp.sum(jnp.sum(sigma * sigma, axis=0, keepdims=True), axis=1, keepdims=True)
        self.block[...] = sigma * (lax.rsqrt(n * (squares / float(n * n)) + 1e-06) / 2.2)

    def form_gram(self):
        n = self.n
        high, low = halves(self.block[...])
        self.cols[:, pl.ds(0, n)] = high
        self.cols[:, pl.ds(n, n)] = low
        self.rows[pl.ds(0, n)] = high
        self.rows[pl.ds(n, n)] = low
        both = tdot(high, self.rows[...])
        cross = both[:, n:]
        self.gram[pl.ds(0, n)], self.gram[pl.ds(n, n)] = halves(both[:, :n] + (cross + cross.T))

    def apply(self, scale=None):
        n = self.n
        both = bdot(self.gram[pl.ds(0, n)], self.cols[...])
        moved = both[:, :n] + (both[:, n:] + bdot(self.gram[pl.ds(n, n)], self.cols[:, pl.ds(0, n)]))
        value = 1.5 * self.block[...] - 0.5 * moved
        self.block[...] = value if scale is None else value * scale


def site_kernel(place, ops_here, psi, left, right, own_map, counts, own_columns, half_out, source_out, rows, scalars,
                map_sems, *rest):
    c, n = place.chunks, place.states
    groups = []
    for _ in range(2):
        groups.append((rest[:c], rest[c:c + 6], rest[c + 6]))
        rest = rest[c + 7:]
    (lefts, rights, block, envs, env_sems, lp_high, lp_low, sigma, first, second, pair, sum_sems,
     quarter, gather_sems, polar_block, cols, doubled, gram, out_sems) = rest
    place.locate()
    p = place

    def load(ref, w):
        slot = w % 2 if isinstance(w, int) else lax.rem(w, 2)
        return pltpu.make_async_copy(ref.at[w], envs.at[slot], env_sems.at[slot])

    load(left, 0).start()
    load(left, 1).start()
    place.greet()
    maps = Maps(place, own_map, rows, scalars, map_sems)

    def fetch_of(piece, group):
        held, (stage, up, down, across, within, local), landed = group
        return Fetch(place, maps, piece, held, stage, landed, up, down, across, within, local)

    fetch = fetch_of(lambda j, y: psi.at[pl.ds((p.o * p.ny + y) * p.rows, p.rows), pl.ds(j * LANES, LANES)], groups[0])
    again = fetch_of(lambda j, y: quarter.at[pl.ds(y * p.rows, p.rows), pl.ds(j * LANES, LANES)], groups[1])
    maps.start()
    for j in range(c):
        fetch.begin(j)
    for j in range(min(AHEAD, c)):
        fetch.send_own(j)
    count = counts[0, 0]
    sigma[...] = jnp.zeros((n, n), F32)
    block[pl.ds(n, n), pl.ds(LANES, LANES)] = jnp.zeros((n, LANES), BF16)

    def at(index, events):
        for turn, event in events:
            pl.when(index == turn)(event)

    def line(which, *steps):
        def event():
            for j, k in steps:
                if j < c:
                    which.send_own(j) if k == 0 else which.forward(j, k)
        return event

    def turn_in(which, j):
        def event():
            if j < c:
                which.forward(j, p.nz - 1)
                which.hand_out(j)
        return event

    def middle(j):
        return [(j, k) for k in range(2, p.nz - 1)]

    def convert_left(w, carry):
        load(left, w).wait()
        high, low = halves(envs[lax.rem(w, 2)])
        rows_of = pl.ds(pl.multiple_of(w * n, n), n)
        lefts[rows_of, pl.ds(0, n)] = high
        lefts[rows_of, pl.ds(n, n)] = low

        @pl.when(w < ops_here - 2)
        def _():
            load(left, w + 2).start()

        @pl.when(w >= ops_here - 2)
        def _():
            load(right, w + 2 - ops_here).start()

        at(w, [(1, line(fetch, (0, 1))), (2, line(fetch, (AHEAD, 0), (1, 1))), (2, maps.finish)])
        return carry

    def convert_right(w, carry):
        load(right, w).wait()
        high, low = halves(envs[lax.rem(w, 2)] * (w < count).astype(F32))
        for j in range(c):
            rows_of = pl.ds(pl.multiple_of((j * ops_here + w) * LANES, LANES), LANES)
            rights[rows_of, pl.ds(0, n)] = high[j * LANES:(j + 1) * LANES]
            rights[rows_of, pl.ds(n, n)] = low[j * LANES:(j + 1) * LANES]

        @pl.when(w < ops_here - 2)
        def _():
            load(right, w + 2).start()

        at(w, [(0, line(fetch, *middle(0))), (1, line(fetch, (AHEAD + 1, 0), (2, 1))), (3, line(fetch, *middle(1)))])
        return carry

    lax.fori_loop(0, ops_here, convert_left, 0)
    lax.fori_loop(0, ops_here, convert_right, 0)
    for j in range(AHEAD + 2, c):
        fetch.send_own(j)
    turn_in(fetch, 0)()

    def products(j, carry):
        for turn in range(c):
            @pl.when(j == turn)
            def _():
                line(fetch, (turn + 3, 1), *middle(turn + 2))()
                if turn < c - 2:
                    turn_in(fetch, turn + 1)()
                fetch.receive(turn)

        high, low = halves(fetch.landed[j])
        block[pl.ds(0, n), pl.ds(0, LANES)] = high
        block[pl.ds(n, n), pl.ds(0, LANES)] = high
        block[pl.ds(0, n), pl.ds(LANES, LANES)] = low
        for w in range(ops_here):
            both = bdot(lefts[pl.ds(w * n, n)], block[...])
            high, low = halves(both[:, :LANES] + both[:, LANES:])
            lp_high[:, pl.ds(w * LANES, LANES)] = high
            lp_low[:, pl.ds(w * LANES, LANES)] = low

        @pl.when(j == max(c - 3, 0))
        def _():
            if c > 1:
                turn_in(fetch, c - 1)()

        deep = pl.ds(pl.multiple_of(j * ops_here * LANES, LANES), ops_here * LANES)
        both = bdot(lp_high[...], rights[deep])
        sigma[...] += both[:, :n] + (both[:, n:] + bdot(lp_low[...], rights[deep, pl.ds(0, n)]))
        return carry

    lax.fori_loop(0, c, products, 0)

    side, core = p.o // CORES, lax.rem(p.o, CORES)
    mate = side * CORES + 1 - core
    facing = (1 - side) * CORES + core
    across_mate = (1 - side) * CORES + 1 - core
    q = p.quarter

    def swap_cores(i, far):
        rows_of = (far * CORES + 1 - core) * q
        return pltpu.make_async_remote_copy(
            sigma.at[pl.ds(rows_of, q)], first.at[i], sum_sems.at[0, i], sum_sems.at[1, i],
            device_id=(p.s, mate), device_id_type=MESH)

    for i, far in ((0, 1 - side), (1, side)):
        swap_cores(i, far).start()
    swap_cores(0, 1 - side).wait_recv()
    pair[...] = sigma[pl.ds(((1 - side) * CORES + core) * q, q)] + first[0]
    over = pltpu.make_async_remote_copy(
        pair, second, sum_sems.at[0, 2], sum_sems.at[1, 2], device_id=(p.s, facing), device_id_type=MESH)
    over.start()
    swap_cores(1, side).wait_recv()
    over.wait_recv()
    quarter[...] = sigma[pl.ds(p.o * q, q)] + first[1] + second[...]
    for i, far in ((0, 1 - side), (1, side)):
        swap_cores(i, far).wait_send()
    over.wait_send()

    whole = polar_block
    polar = Polar(n, whole, cols, doubled, gram)

    def gather(i, sender, target):
        rows_of = pl.ds(sender * q, q)
        source = quarter if i < 2 else whole.at[rows_of]
        return pltpu.make_async_remote_copy(
            source, whole.at[rows_of], gather_sems.at[0, i], gather_sems.at[1, i],
            device_id=(p.s, target), device_id_type=MESH)

    gather(1, p.o, facing).start()
    gather(0, p.o, mate).start()
    for j in range(c):
        again.begin(j)
    whole[pl.ds(p.o * q, q)] = quarter[...]
    for j in range(min(AHEAD, c)):
        again.send_own(j)
    line(again, (0, 1), (AHEAD, 0), (1, 1))()
    gather(1, facing, facing).wait_recv()
    gather(2, facing, mate).start()
    line(again, *middle(0))()
    for j in range(AHEAD + 1, c):
        again.send_own(j)
    gather(0, mate, mate).wait_recv()
    gather(2, across_mate, mate).wait_recv()
    gather(2, facing, mate).wait_send()
    polar.normalise(whole[...])

    def group(turn):
        def event():
            line(again, (turn + 1, 1), *middle(turn))()
            turn_in(again, turn - 1)()
        return event

    def own_step(step, carry):
        polar.form_gram()
        polar.apply()
        at(step, [(turn - 1, group(turn)) for turn in range(1, min(c, POLAR) + 1)])
        return carry

    lax.fori_loop(0, POLAR, own_step, 0)
    for turn in range(POLAR + 1, c + 1):
        group(turn)()
    tensor = (whole[...] * math.sqrt(n)).T
    whole[...] = tensor
    own_columns[...] = whole[pl.ds(pl.multiple_of(p.o * q, q), q)]
    gram[pl.ds(0, n)], gram[pl.ds(n, n)] = halves(tensor)

    def half_rotate(w, carry):
        rows_of = pl.ds(pl.multiple_of(w * n, n), n)
        both = bdot(gram[pl.ds(0, n)], lefts[rows_of])
        turned = both[:, :n] + (both[:, n:] + bdot(gram[pl.ds(n, n)], lefts[rows_of, pl.ds(0, n)]))
        rights[rows_of, pl.ds(0, n)], rights[rows_of, pl.ds(n, n)] = halves(turned)
        pltpu.make_async_copy(rights.at[rows_of], half_out.at[rows_of], out_sems.at[w]).start()
        return carry

    lax.fori_loop(0, ops_here, half_rotate, 0)
    for j in range(c):
        again.receive(j)
    save = pltpu.make_async_copy(again.landed, source_out, out_sems.at[ops_here])
    save.start()
    for w in range(ops_here):
        rows_of = pl.ds(w * n, n)
        pltpu.make_async_copy(rights.at[rows_of], half_out.at[rows_of], out_sems.at[w]).wait()
    fetch.drain()
    again.drain()
    gather(1, p.o, facing).wait_send()
    gather(0, p.o, mate).wait_send()
    save.wait()


def last_kernel(n, ops_here, chunks, source, half, columns, own_columns, rotated, block, cols, doubled, gram, halves_in,
                products, in_sems, out_sems):
    def load(w):
        at = pl.ds(w * n, n)
        return pltpu.make_async_copy(half.at[at], halves_in.at[at], in_sems.at[w])

    def store(w):
        return pltpu.make_async_copy(products.at[w], rotated.at[w], out_sems.at[w])

    for w in range(ops_here):
        load(w).start()
    own_columns[...] = columns[...]
    polar = Polar(n, block, cols, doubled, gram)
    polar.normalise(jnp.concatenate([source[j] for j in range(chunks)], axis=1))

    def step(_, carry):
        polar.form_gram()
        polar.apply()
        return carry

    lax.fori_loop(0, POLAR, step, 0)
    high, low = halves(block[...] * math.sqrt(n))
    cols[:, pl.ds(0, n)] = high
    cols[:, pl.ds(n, n)] = low

    def rotate(w, carry):
        load(w).wait()
        rows_of = pl.ds(pl.multiple_of(w * n, n), n)
        both = bdot(halves_in[rows_of, pl.ds(0, n)], cols[...])
        products[w] = both[:, :n] + (both[:, n:] + bdot(halves_in[rows_of, pl.ds(n, n)], cols[:, pl.ds(0, n)]))
        store(w).start()
        return carry

    lax.fori_loop(0, ops_here, rotate, 0)
    for w in range(ops_here):
        store(w).wait()


def vmem():
    return pl.BlockSpec(memory_space=pltpu.VMEM)


def anywhere():
    return pl.BlockSpec(memory_space=pl.ANY)


def shards_planes(place, wavefunction, left_env, right_env, shift_map, op_counts):
    c, n, q, ops_here = place.chunks, place.states, place.quarter, left_env.shape[1]
    own_map = jnp.pad(shift_map, ((0, 0), (0, LANES - shift_map.shape[1])))
    fetches = []
    for _ in range(2):
        held, stage, *sems = Fetch.scratch(place)
        fetches += [*held, stage, *sems, pltpu.VMEM((c, n, LANES), F32)]
    columns, half, source = pl.pallas_call(
        functools.partial(site_kernel, place, ops_here),
        out_shape=(
            jax.ShapeDtypeStruct((q, n), F32),
            jax.ShapeDtypeStruct((ops_here * n, 2 * n), BF16),
            jax.ShapeDtypeStruct((c, n, LANES), F32),
        ),
        in_specs=[vmem(), anywhere(), anywhere(), vmem(), pl.BlockSpec(memory_space=pltpu.SMEM)],
        out_specs=(vmem(), anywhere(), anywhere()),
        scratch_shapes=[
            *Maps.scratch(place), *fetches,
            pltpu.VMEM((ops_here * n, 2 * n), BF16),
            pltpu.VMEM((ops_here * n, 2 * n), BF16),
            pltpu.VMEM((2 * n, 2 * LANES), BF16),
            pltpu.VMEM((2, n, n), F32),
            pltpu.SemaphoreType.DMA((2,)),
            pltpu.VMEM((n, ops_here * LANES), BF16),
            pltpu.VMEM((n, ops_here * LANES), BF16),
            pltpu.VMEM((n, n), F32),
            pltpu.VMEM((2, q, n), F32),
            pltpu.VMEM((q, n), F32),
            pltpu.VMEM((q, n), F32),
            pltpu.SemaphoreType.DMA((2, 3)),
            pltpu.VMEM((q, n), F32),
            pltpu.SemaphoreType.DMA((2, 3)),
            pltpu.VMEM((n, n), F32),
            *Polar.scratch(n),
            pltpu.SemaphoreType.DMA((ops_here + 1,)),
        ],
        compiler_params=pltpu.CompilerParams(collective_id=0, has_side_effects=True, vmem_limit_bytes=60 * 2**20),
    )(wavefunction[0], left_env[0], right_env[0], own_map, op_counts)
    own_columns, rotated = pl.pallas_call(
        functools.partial(last_kernel, n, ops_here, c),
        out_shape=(jax.ShapeDtypeStruct((q, n), F32), jax.ShapeDtypeStruct((ops_here, n, n), F32)),
        in_specs=[vmem(), anywhere(), vmem()],
        out_specs=(vmem(), anywhere()),
        scratch_shapes=[
            pltpu.VMEM((n, n), F32),
            *Polar.scratch(n),
            pltpu.VMEM((ops_here * n, 2 * n), BF16),
            pltpu.VMEM((ops_here, n, n), F32),
            pltpu.SemaphoreType.DMA((ops_here,)),
            pltpu.SemaphoreType.DMA((ops_here,)),
        ],
        compiler_params=pltpu.CompilerParams(vmem_limit_bytes=60 * 2**20),
    )(source, half, columns)
    return own_columns.T[None], rotated[None]


def line_split(sector_count):
    rows = 1
    while rows * 2 * rows * 2 <= sector_count and sector_count % (rows * 2) == 0:
        rows *= 2
    return rows


def solution(mesh):
    def shards(wavefunction, left_env, right_env, shift_map, op_counts):
        nsec, nops = mesh.shape["sector"], mesh.shape["ops"]
        states = wavefunction.shape[1]
        ny = line_split(nsec)
        fits = nops == 2 * CORES and ny == 2 and states % LANES == 0 and states % (nops * ny * SUBLANES) == 0
        if not fits:
            return shards_general(wavefunction, left_env, right_env, shift_map, op_counts)
        place = Place(nsec, nops, ny, states)
        return shards_planes(place, wavefunction, left_env, right_env, shift_map, op_counts)

    return jax.shard_map(
        shards,
        mesh=mesh,
        in_specs=(
            P("sector", None, None),
            P("sector", "ops", None, None),
            P("sector", "ops", None, None),
            P("ops", None),
            P("ops", "sector"),
        ),
        out_specs=(P("sector", None, "ops"), P("sector", "ops", None, None)),
        check_vma=False,
    )
```

profile of v0, /device:TPU:0, one launch (start us, length us, event | category | flops | bytes accessed | tf_op | source)
XLA Modules:
  0.0 144.3 jit_solution(9769563510156090497)
XLA Ops:
  1.3 1.2 pad.4.own_map
  2.4 110.0 %shard_map.68 = (f32[160,640]{1,0:T(8,128)}, bf16[2560,1280]{1,0:T(8,128)(2,1)}, f32[5,640,128]{2,1,0:T(8,128)}) custom-call(f32[640,640]{1,0:T(8,128)} %bitcast.9, f32[4,640,640]{2,1,0:T(8,128)} %bitcast.7, f32[4,640,640]{2,1,0:T(8,128)} %bitcast.8, s32[1,128]{1,0:T(1,128)} %pad.4.own_map, s32[1,1]{1,0:T(1,128)S(6)} %copy.7.counts), custom_call_target="tpu_custom_call" | custom-call | tf_op jit(solution)/shard_map/pallas_call | solution.py:641
  112.5 31.6 %shard_map.69 = (f32[160,640]{1,0:T(8,128)}, f32[4,640,640]{2,1,0:T(8,128)}) custom-call(f32[5,640,128]{2,1,0:T(8,128)} %get-tuple-element.7.source, bf16[2560,1280]{1,0:T(8,128)(2,1)} %get-tuple-element.8.half, f32[160,640]{1,0:T(8,128)} %get-tuple-element.9.columns), custom_call_target="tpu_custom_call" | custom-call | tf_op jit(solution)/shard_map/pallas_call | solution.py:672
where the time goes:
time: 144 us
  Pallas kernels  142 us (99%)
  between operations  1.45 us (1%)
    pallas_call x1, Pallas kernels, shards_planes(): pl.pallas_call(functools.partial(site_kernel, place, ops_here), out_shape...  110 us
    pallas_call x1, Pallas kernels, shards_planes(): pl.pallas_call(functools.partial(last_kernel, n, ops_here, c), out_shape=...  31.6 us

commit v1 on v0

--- a/solution.py
+++ b/solution.py
@@ -172,16 +172,25 @@
 
 
 class Maps:
-    def __init__(self, place, own_ref, rows_ref, scalars_ref, sems):
-        self.place, self.own, self.rows, self.scalars, self.sems = place, own_ref, rows_ref, scalars_ref, sems
+    def __init__(self, place, table, own_ref, rows_ref, scalars_ref, sems):
+        self.place, self.table = place, table
+        self.own, self.rows, self.scalars, self.sems = own_ref, rows_ref, scalars_ref, sems
 
     @staticmethod
     def scratch(place):
         return [
+            pltpu.VMEM((1, LANES), jnp.int32),
             pltpu.VMEM((place.nops, 1, LANES), jnp.int32),
             pltpu.SMEM((place.nops, 1, LANES), jnp.int32),
             pltpu.SemaphoreType.DMA((3, place.nops)),
         ]
+
+    def write(self):
+        lane = lax.broadcasted_iota(jnp.int32, (1, LANES), 1)
+        row = jnp.zeros((1, LANES), jnp.int32)
+        for sector in range(self.place.nsec):
+            row = jnp.where(lane == sector, self.table[0, sector], row)
+        self.own[...] = row
 
     def copy(self, offset, sign):
         p = self.place
@@ -306,6 +315,8 @@
                 self.landed[j, pl.ds(p.part * p.rows, p.rows)] = picked
             else:
                 self.stage[j, index] = picked
+        for index in order:
+            if index:
                 self.within_copy(j, index, 1).start()
 
     def receive(self, j):
@@ -361,8 +372,8 @@
         self.block[...] = value if scale is None else value * scale
 
 
-def site_kernel(place, ops_here, psi, left, right, own_map, counts, own_columns, half_out, source_out, rows, scalars,
-                map_sems, *rest):
+def site_kernel(place, ops_here, psi, left, right, table, counts, own_columns, half_out, source_out, map_row, rows,
+                scalars, map_sems, *rest):
     c, n = place.chunks, place.states
     groups = []
     for _ in range(2):
@@ -379,8 +390,9 @@
 
     load(left, 0).start()
     load(left, 1).start()
+    maps = Maps(place, table, map_row, rows, scalars, map_sems)
+    maps.write()
     place.greet()
-    maps = Maps(place, own_map, rows, scalars, map_sems)
 
     def fetch_of(piece, group):
         held, (stage, up, down, across, within, local), landed = group
@@ -494,68 +506,77 @@
     across_mate = (1 - side) * CORES + 1 - core
     q = p.quarter
 
-    def swap_cores(i, far):
-        rows_of = (far * CORES + 1 - core) * q
-        return pltpu.make_async_remote_copy(
-            sigma.at[pl.ds(rows_of, q)], first.at[i], sum_sems.at[0, i], sum_sems.at[1, i],
-            device_id=(p.s, mate), device_id_type=MESH)
-
-    for i, far in ((0, 1 - side), (1, side)):
-        swap_cores(i, far).start()
-    swap_cores(0, 1 - side).wait_recv()
-    pair[...] = sigma[pl.ds(((1 - side) * CORES + core) * q, q)] + first[0]
-    over = pltpu.make_async_remote_copy(
-        pair, second, sum_sems.at[0, 2], sum_sems.at[1, 2], device_id=(p.s, facing), device_id_type=MESH)
-    over.start()
-    swap_cores(1, side).wait_recv()
-    over.wait_recv()
-    quarter[...] = sigma[pl.ds(p.o * q, q)] + first[1] + second[...]
-    for i, far in ((0, 1 - side), (1, side)):
-        swap_cores(i, far).wait_send()
-    over.wait_send()
-
     whole = polar_block
     polar = Polar(n, whole, cols, doubled, gram)
 
-    def gather(i, sender, target):
-        rows_of = pl.ds(sender * q, q)
-        source = quarter if i < 2 else whole.at[rows_of]
+    def swap_cores(i, far, j):
+        rows_of, at_cols = pl.ds((far * CORES + 1 - core) * q, q), pl.ds(j * LANES, LANES)
         return pltpu.make_async_remote_copy(
-            source, whole.at[rows_of], gather_sems.at[0, i], gather_sems.at[1, i],
+            sigma.at[rows_of, at_cols], first.at[i, :, at_cols], sum_sems.at[0, i, j], sum_sems.at[1, i, j],
+            device_id=(p.s, mate), device_id_type=MESH)
+
+    def over(j):
+        at_cols = pl.ds(j * LANES, LANES)
+        return pltpu.make_async_remote_copy(
+            pair.at[:, at_cols], second.at[:, at_cols], sum_sems.at[0, 2, j], sum_sems.at[1, 2, j],
+            device_id=(p.s, facing), device_id_type=MESH)
+
+    def gather(i, sender, target, j):
+        rows_of, at_cols = pl.ds(sender * q, q), pl.ds(j * LANES, LANES)
+        source = quarter.at[:, at_cols] if i < 2 else whole.at[rows_of, at_cols]
+        return pltpu.make_async_remote_copy(
+            source, whole.at[rows_of, at_cols], gather_sems.at[0, i, j], gather_sems.at[1, i, j],
             device_id=(p.s, target), device_id_type=MESH)
 
-    gather(1, p.o, facing).start()
-    gather(0, p.o, mate).start()
     for j in range(c):
-        again.begin(j)
-    whole[pl.ds(p.o * q, q)] = quarter[...]
-    for j in range(min(AHEAD, c)):
-        again.send_own(j)
-    line(again, (0, 1), (AHEAD, 0), (1, 1))()
-    gather(1, facing, facing).wait_recv()
-    gather(2, facing, mate).start()
-    line(again, *middle(0))()
-    for j in range(AHEAD + 1, c):
-        again.send_own(j)
-    gather(0, mate, mate).wait_recv()
-    gather(2, across_mate, mate).wait_recv()
-    gather(2, facing, mate).wait_send()
+        swap_cores(0, 1 - side, j).start()
+        swap_cores(1, side, j).start()
+    for j in range(c + 1):
+        if j < c:
+            at_cols = pl.ds(j * LANES, LANES)
+            swap_cores(0, 1 - side, j).wait_recv()
+            pair[:, at_cols] = sigma[pl.ds(((1 - side) * CORES + core) * q, q), at_cols] + first[0, :, at_cols]
+        if j:
+            over(j - 1).start()
+    for j in range(c + 1):
+        if j < c:
+            at_cols = pl.ds(j * LANES, LANES)
+            swap_cores(1, side, j).wait_recv()
+            over(j).wait_recv()
+            quarter[:, at_cols] = sigma[pl.ds(p.o * q, q), at_cols] + first[1, :, at_cols] + second[:, at_cols]
+            whole[pl.ds(p.o * q, q), at_cols] = quarter[:, at_cols]
+        if j:
+            again.begin(j - 1)
+            gather(1, p.o, facing, j - 1).start()
+            gather(0, p.o, mate, j - 1).start()
+        if j > 1:
+            again.send_own(j - 2)
+    again.send_own(c - 1)
+    for j in range(c):
+        gather(1, facing, facing, j).wait_recv()
+        gather(2, facing, mate, j).start()
+        if j < 2:
+            line(again, (j, 1), *middle(j))()
+    for j in range(c):
+        gather(0, mate, mate, j).wait_recv()
+        gather(2, across_mate, mate, j).wait_recv()
+        gather(2, facing, mate, j).wait_send()
     polar.normalise(whole[...])
 
     def group(turn):
         def event():
-            line(again, (turn + 1, 1), *middle(turn))()
-            turn_in(again, turn - 1)()
+            line(again, (turn + 2, 1), *middle(turn + 2))()
+            turn_in(again, turn)()
         return event
 
     def own_step(step, carry):
         polar.form_gram()
         polar.apply()
-        at(step, [(turn - 1, group(turn)) for turn in range(1, min(c, POLAR) + 1)])
+        at(step, [(turn, group(turn)) for turn in range(min(c, POLAR))])
         return carry
 
     lax.fori_loop(0, POLAR, own_step, 0)
-    for turn in range(POLAR + 1, c + 1):
+    for turn in range(POLAR, c):
         group(turn)()
     tensor = (whole[...] * math.sqrt(n)).T
     whole[...] = tensor
@@ -580,8 +601,12 @@
         pltpu.make_async_copy(rights.at[rows_of], half_out.at[rows_of], out_sems.at[w]).wait()
     fetch.drain()
     again.drain()
-    gather(1, p.o, facing).wait_send()
-    gather(0, p.o, mate).wait_send()
+    for j in range(c):
+        swap_cores(0, 1 - side, j).wait_send()
+        swap_cores(1, side, j).wait_send()
+        over(j).wait_send()
+        gather(1, p.o, facing, j).wait_send()
+        gather(0, p.o, mate, j).wait_send()
     save.wait()
 
 
@@ -627,13 +652,16 @@
     return pl.BlockSpec(memory_space=pltpu.VMEM)
 
 
+def scalar():
+    return pl.BlockSpec(memory_space=pltpu.SMEM)
+
+
 def anywhere():
     return pl.BlockSpec(memory_space=pl.ANY)
 
 
 def shards_planes(place, wavefunction, left_env, right_env, shift_map, op_counts):
     c, n, q, ops_here = place.chunks, place.states, place.quarter, left_env.shape[1]
-    own_map = jnp.pad(shift_map, ((0, 0), (0, LANES - shift_map.shape[1])))
     fetches = []
     for _ in range(2):
         held, stage, *sems = Fetch.scratch(place)
@@ -645,7 +673,7 @@
             jax.ShapeDtypeStruct((ops_here * n, 2 * n), BF16),
             jax.ShapeDtypeStruct((c, n, LANES), F32),
         ),
-        in_specs=[vmem(), anywhere(), anywhere(), vmem(), pl.BlockSpec(memory_space=pltpu.SMEM)],
+        in_specs=[anywhere(), anywhere(), anywhere(), scalar(), scalar()],
         out_specs=(vmem(), anywhere(), anywhere()),
         scratch_shapes=[
             *Maps.scratch(place), *fetches,
@@ -660,15 +688,15 @@
             pltpu.VMEM((2, q, n), F32),
             pltpu.VMEM((q, n), F32),
             pltpu.VMEM((q, n), F32),
-            pltpu.SemaphoreType.DMA((2, 3)),
+            pltpu.SemaphoreType.DMA((2, 3, c)),
             pltpu.VMEM((q, n), F32),
-            pltpu.SemaphoreType.DMA((2, 3)),
+            pltpu.SemaphoreType.DMA((2, 3, c)),
             pltpu.VMEM((n, n), F32),
             *Polar.scratch(n),
             pltpu.SemaphoreType.DMA((ops_here + 1,)),
         ],
         compiler_params=pltpu.CompilerParams(collective_id=0, has_side_effects=True, vmem_limit_bytes=60 * 2**20),
-    )(wavefunction[0], left_env[0], right_env[0], own_map, op_counts)
+    )(wavefunction[0], left_env[0], right_env[0], shift_map, op_counts)
     own_columns, rotated = pl.pallas_call(
         functools.partial(last_kernel, n, ops_here, c),
         out_shape=(jax.ShapeDtypeStruct((q, n), F32), jax.ShapeDtypeStruct((ops_here, n, n), F32)),

time: 144 us -> 155 us (1.076)
  Pallas kernels: 142 us -> 153 us
    pallas_call x1, Pallas kernels: 110 us -> 122 us  [shards_planes(): pl.pallas_call(functools.partial(site_kernel, place, ops_here), out_shape...]
where the time goes in v1:
time: 155 us
  Pallas kernels  153 us (99%)
    pallas_call x1, Pallas kernels, shards_planes(): pl.pallas_call(functools.partial(site_kernel, place, ops_here), out_shape...  122 us
    pallas_call x1, Pallas kernels, shards_planes(): pl.pallas_call(functools.partial(last_kernel, n, ops_here, c), out_shape=...  31.6 us

profile of v1, /device:TPU:0, one launch (start us, length us, event | category | flops | bytes accessed | tf_op | source)
XLA Modules:
  0.0 154.6 jit_solution(315791586046201212)
XLA Ops:
  1.3 121.5 %shard_map.68 = (f32[160,640]{1,0:T(8,128)}, bf16[2560,1280]{1,0:T(8,128)(2,1)}, f32[5,640,128]{2,1,0:T(8,128)}) custom-call(f32[640,640]{1,0:T(8,128)} %bitcast.9, f32[4,640,640]{2,1,0:T(8,128)} %bitcast.7, f32[4,640,640]{2,1,0:T(8,128)} %bitcast.8, s32[1,8]{1,0:T(1,128)} %table.1, s32[1,1]{1,0:T(1,128)S(6)} %copy.7.counts), custom_call_target="tpu_custom_call" | custom-call | tf_op jit(solution)/shard_map/pallas_call | solution.py:669
  122.8 31.6 %shard_map.69 = (f32[160,640]{1,0:T(8,128)}, f32[4,640,640]{2,1,0:T(8,128)}) custom-call(f32[5,640,128]{2,1,0:T(8,128)} %get-tuple-element.7.source, bf16[2560,1280]{1,0:T(8,128)(2,1)} %get-tuple-element.8.half, f32[160,640]{1,0:T(8,128)} %get-tuple-element.9.columns), custom_call_target="tpu_custom_call" | custom-call | tf_op jit(solution)/shard_map/pallas_call | solution.py:700

commit v2 on v1

--- a/solution.py
+++ b/solution.py
@@ -555,8 +555,8 @@
     for j in range(c):
         gather(1, facing, facing, j).wait_recv()
         gather(2, facing, mate, j).start()
-        if j < 2:
-            line(again, (j, 1), *middle(j))()
+        again.forward(j, 1)
+    line(again, *middle(0), *middle(1))()
     for j in range(c):
         gather(0, mate, mate, j).wait_recv()
         gather(2, across_mate, mate, j).wait_recv()
@@ -565,8 +565,9 @@
 
     def group(turn):
         def event():
-            line(again, (turn + 2, 1), *middle(turn + 2))()
-            turn_in(again, turn)()
+            line(again, *middle(turn + 2))()
+            if turn:
+                turn_in(again, turn - 1)()
         return event
 
     def own_step(step, carry):
@@ -589,6 +590,7 @@
         turned = both[:, :n] + (both[:, n:] + bdot(gram[pl.ds(n, n)], lefts[rows_of, pl.ds(0, n)]))
         rights[rows_of, pl.ds(0, n)], rights[rows_of, pl.ds(n, n)] = halves(turned)
         pltpu.make_async_copy(rights.at[rows_of], half_out.at[rows_of], out_sems.at[w]).start()
+        at(w, [(0, turn_in(again, c - 1))])
         return carry
 
     lax.fori_loop(0, ops_here, half_rotate, 0)

time: 155 us -> 141 us (0.910)
  Pallas kernels: 153 us -> 140 us
    pallas_call x1, Pallas kernels: 122 us -> 108 us  [shards_planes(): pl.pallas_call(functools.partial(site_kernel, place, ops_here), out_shape...]
where the time goes in v2:
time: 141 us
  Pallas kernels  140 us (99%)
  between operations  1.45 us (1%)
    pallas_call x1, Pallas kernels, shards_planes(): pl.pallas_call(functools.partial(site_kernel, place, ops_here), out_shape...  108 us
    pallas_call x1, Pallas kernels, shards_planes(): pl.pallas_call(functools.partial(last_kernel, n, ops_here, c), out_shape=...  31.6 us

profile of v2, /device:TPU:0, one launch (start us, length us, event | category | flops | bytes accessed | tf_op | source)
XLA Modules:
  0.0 141.0 jit_solution(3757676716500916879)
XLA Ops:
  1.3 107.9 %shard_map.68 = (f32[160,640]{1,0:T(8,128)}, bf16[2560,1280]{1,0:T(8,128)(2,1)}, f32[5,640,128]{2,1,0:T(8,128)}) custom-call(f32[640,640]{1,0:T(8,128)} %bitcast.9, f32[4,640,640]{2,1,0:T(8,128)} %bitcast.7, f32[4,640,640]{2,1,0:T(8,128)} %bitcast.8, s32[1,8]{1,0:T(1,128)} %table.1, s32[1,1]{1,0:T(1,128)S(6)} %copy.7.counts), custom_call_target="tpu_custom_call" | custom-call | tf_op jit(solution)/shard_map/pallas_call | solution.py:671
  109.2 31.6 %shard_map.69 = (f32[160,640]{1,0:T(8,128)}, f32[4,640,640]{2,1,0:T(8,128)}) custom-call(f32[5,640,128]{2,1,0:T(8,128)} %get-tuple-element.7.source, bf16[2560,1280]{1,0:T(8,128)(2,1)} %get-tuple-element.8.half, f32[160,640]{1,0:T(8,128)} %get-tuple-element.9.columns), custom_call_target="tpu_custom_call" | custom-call | tf_op jit(solution)/shard_map/pallas_call | solution.py:702

commit v3 on v2

--- a/solution.py
+++ b/solution.py
@@ -12,6 +12,8 @@
 LANES, SUBLANES = 128, 8
 CORES = 2
 AHEAD = 3
+WIDE = 256
+PAIR = 2
 MESH = pl.DeviceIdType.MESH
 F32, BF16 = jnp.float32, jnp.bfloat16
 
@@ -380,7 +382,7 @@
         groups.append((rest[:c], rest[c:c + 6], rest[c + 6]))
         rest = rest[c + 7:]
     (lefts, rights, block, envs, env_sems, lp_high, lp_low, sigma, first, second, pair, sum_sems,
-     quarter, gather_sems, polar_block, cols, doubled, gram, out_sems) = rest
+     quarter, gather_sems, polar_block, cols, doubled, gram, stacked, turned, out_sems) = rest
     place.locate()
     p = place
 
@@ -436,6 +438,9 @@
         rows_of = pl.ds(pl.multiple_of(w * n, n), n)
         lefts[rows_of, pl.ds(0, n)] = high
         lefts[rows_of, pl.ds(n, n)] = low
+        beside = pl.ds(pl.multiple_of(lax.rem(w, PAIR) * n, LANES), n)
+        for third, value in enumerate((high, low, high)):
+            stacked[w // PAIR, pl.ds(third * n, n), beside] = value
 
         @pl.when(w < ops_here - 2)
         def _():
@@ -556,7 +561,7 @@
         gather(1, facing, facing, j).wait_recv()
         gather(2, facing, mate, j).start()
         again.forward(j, 1)
-    line(again, *middle(0), *middle(1))()
+    line(again, *middle(0))()
     for j in range(c):
         gather(0, mate, mate, j).wait_recv()
         gather(2, across_mate, mate, j).wait_recv()
@@ -565,7 +570,7 @@
 
     def group(turn):
         def event():
-            line(again, *middle(turn + 2))()
+            line(again, *(middle(1) if turn == 0 else []), *middle(turn + 2))()
             if turn:
                 turn_in(again, turn - 1)()
         return event
@@ -582,18 +587,22 @@
     tensor = (whole[...] * math.sqrt(n)).T
     whole[...] = tensor
     own_columns[...] = whole[pl.ds(pl.multiple_of(p.o * q, q), q)]
-    gram[pl.ds(0, n)], gram[pl.ds(n, n)] = halves(tensor)
-
-    def half_rotate(w, carry):
-        rows_of = pl.ds(pl.multiple_of(w * n, n), n)
-        both = bdot(gram[pl.ds(0, n)], lefts[rows_of])
-        turned = both[:, :n] + (both[:, n:] + bdot(gram[pl.ds(n, n)], lefts[rows_of, pl.ds(0, n)]))
-        rights[rows_of, pl.ds(0, n)], rights[rows_of, pl.ds(n, n)] = halves(turned)
-        pltpu.make_async_copy(rights.at[rows_of], half_out.at[rows_of], out_sems.at[w]).start()
-        at(w, [(0, turn_in(again, c - 1))])
+    high, low = halves(tensor)
+    turned[:, pl.ds(0, n)] = high
+    turned[:, pl.ds(n, n)] = high
+    turned[:, pl.ds(2 * n, n)] = low
+
+    def half_rotate(pair, carry):
+        both = bdot(turned[...], stacked[pair])
+        for i in range(PAIR):
+            w = pair * PAIR + i
+            rows_of = pl.ds(pl.multiple_of(w * n, n), n)
+            rights[rows_of, pl.ds(0, n)], rights[rows_of, pl.ds(n, n)] = halves(both[:, i * n:(i + 1) * n])
+            pltpu.make_async_copy(rights.at[rows_of], half_out.at[rows_of], out_sems.at[w]).start()
+        at(pair, [(0, turn_in(again, c - 1))])
         return carry
 
-    lax.fori_loop(0, ops_here, half_rotate, 0)
+    lax.fori_loop(0, ops_here // PAIR, half_rotate, 0)
     for j in range(c):
         again.receive(j)
     save = pltpu.make_async_copy(again.landed, source_out, out_sems.at[ops_here])
@@ -612,8 +621,8 @@
     save.wait()
 
 
-def last_kernel(n, ops_here, chunks, source, half, columns, own_columns, rotated, block, cols, doubled, gram, halves_in,
-                products, in_sems, out_sems):
+def last_kernel(n, ops_here, chunks, source, half, columns, own_columns, rotated, block, cols, doubled, gram, halves_in, double,
+                tail, products, in_sems, out_sems):
     def load(w):
         at = pl.ds(w * n, n)
         return pltpu.make_async_copy(half.at[at], halves_in.at[at], in_sems.at[w])
@@ -633,15 +642,26 @@
         return carry
 
     lax.fori_loop(0, POLAR, step, 0)
+    wide = n - n % WIDE
+    rest = n - wide
     high, low = halves(block[...] * math.sqrt(n))
-    cols[:, pl.ds(0, n)] = high
-    cols[:, pl.ds(n, n)] = low
+    double[pl.ds(0, n)] = high[:, :wide]
+    double[pl.ds(n, n)] = high[:, :wide]
+    cols[:, pl.ds(0, wide)] = low[:, :wide]
+    if rest:
+        tail[pl.ds(0, n), pl.ds(0, rest)] = high[:, wide:]
+        tail[pl.ds(0, n), pl.ds(rest, rest)] = low[:, wide:]
+        tail[pl.ds(n, n), pl.ds(0, rest)] = high[:, wide:]
+        tail[pl.ds(n, n), pl.ds(rest, rest)] = jnp.zeros((n, rest), BF16)
 
     def rotate(w, carry):
         load(w).wait()
         rows_of = pl.ds(pl.multiple_of(w * n, n), n)
-        both = bdot(halves_in[rows_of, pl.ds(0, n)], cols[...])
-        products[w] = both[:, :n] + (both[:, n:] + bdot(halves_in[rows_of, pl.ds(n, n)], cols[:, pl.ds(0, n)]))
+        both = halves_in[rows_of]
+        products[w, :, pl.ds(0, wide)] = bdot(both, double[...]) + bdot(both[:, :n], cols[:, pl.ds(0, wide)])
+        if rest:
+            ends = bdot(both, tail[...])
+            products[w, :, pl.ds(wide, rest)] = ends[:, :rest] + ends[:, rest:]
         store(w).start()
         return carry
 
@@ -695,6 +715,8 @@
             pltpu.SemaphoreType.DMA((2, 3, c)),
             pltpu.VMEM((n, n), F32),
             *Polar.scratch(n),
+            pltpu.VMEM((ops_here // PAIR, 3 * n, PAIR * n), BF16),
+            pltpu.VMEM((n, 3 * n), BF16),
             pltpu.SemaphoreType.DMA((ops_here + 1,)),
         ],
         compiler_params=pltpu.CompilerParams(collective_id=0, has_side_effects=True, vmem_limit_bytes=60 * 2**20),
@@ -708,6 +730,8 @@
             pltpu.VMEM((n, n), F32),
             *Polar.scratch(n),
             pltpu.VMEM((ops_here * n, 2 * n), BF16),
+            pltpu.VMEM((2 * n, n - n % WIDE), BF16),
+            pltpu.VMEM((2 * n, 2 * max(n % WIDE, LANES)), BF16),
             pltpu.VMEM((ops_here, n, n), F32),
             pltpu.SemaphoreType.DMA((ops_here,)),
             pltpu.SemaphoreType.DMA((ops_here,)),
@@ -729,7 +753,8 @@
         nsec, nops = mesh.shape["sector"], mesh.shape["ops"]
         states = wavefunction.shape[1]
         ny = line_split(nsec)
-        fits = nops == 2 * CORES and ny == 2 and states % LANES == 0 and states % (nops * ny * SUBLANES) == 0
+        per_group = left_env.shape[1] % PAIR == 0
+        fits = per_group and nops == 2 * CORES and ny == 2 and states % LANES == 0 and states % (nops * ny * SUBLANES) == 0
         if not fits:
             return shards_general(wavefunction, left_env, right_env, shift_map, op_counts)
         place = Place(nsec, nops, ny, states)

time: 141 us -> 138 us (0.979)
  Pallas kernels: 140 us -> 136 us
    pallas_call x1, Pallas kernels: 108 us -> 106 us  [shards_planes(): pl.pallas_call(functools.partial(site_kernel, place, ops_here), out_shape...]
where the time goes in v3:
time: 138 us
  Pallas kernels  136 us (99%)
  between operations  1.45 us (1%)
    pallas_call x1, Pallas kernels, shards_planes(): pl.pallas_call(functools.partial(site_kernel, place, ops_here), out_shape...  106 us
    pallas_call x1, Pallas kernels, shards_planes(): pl.pallas_call(functools.partial(last_kernel, n, ops_here, c), out_shape=...  30.8 us

profile of v3, /device:TPU:0, one launch (start us, length us, event | category | flops | bytes accessed | tf_op | source)
XLA Modules:
  0.0 137.9 jit_solution(10672107905018905584)
XLA Ops:
  1.3 105.6 %shard_map.68 = (f32[160,640]{1,0:T(8,128)}, bf16[2560,1280]{1,0:T(8,128)(2,1)}, f32[5,640,128]{2,1,0:T(8,128)}) custom-call(f32[640,640]{1,0:T(8,128)} %bitcast.9, f32[4,640,640]{2,1,0:T(8,128)} %bitcast.7, f32[4,640,640]{2,1,0:T(8,128)} %bitcast.8, s32[1,8]{1,0:T(1,128)} %table.1, s32[1,1]{1,0:T(1,128)S(6)} %copy.7.counts), custom_call_target="tpu_custom_call" | custom-call | tf_op jit(solution)/shard_map/pallas_call | solution.py:691
  106.9 30.8 %shard_map.69 = (f32[160,640]{1,0:T(8,128)}, f32[4,640,640]{2,1,0:T(8,128)}) custom-call(f32[5,640,128]{2,1,0:T(8,128)} %get-tuple-element.7.source, bf16[2560,1280]{1,0:T(8,128)(2,1)} %get-tuple-element.8.half, f32[160,640]{1,0:T(8,128)} %get-tuple-element.9.columns), custom_call_target="tpu_custom_call" | custom-call | tf_op jit(solution)/shard_map/pallas_call | solution.py:724

commit v4 on v3

--- a/solution.py
+++ b/solution.py
@@ -11,7 +11,7 @@
 POLAR = 5
 LANES, SUBLANES = 128, 8
 CORES = 2
-AHEAD = 3
+AHEAD = 2
 WIDE = 256
 PAIR = 2
 MESH = pl.DeviceIdType.MESH
@@ -474,6 +474,18 @@
         fetch.send_own(j)
     turn_in(fetch, 0)()
 
+    side, core = p.o // CORES, lax.rem(p.o, CORES)
+    mate = side * CORES + 1 - core
+    facing = (1 - side) * CORES + core
+    across_mate = (1 - side) * CORES + 1 - core
+    q = p.quarter
+
+    def swap_cores(i, far, j):
+        rows_of, at_cols = pl.ds((far * CORES + 1 - core) * q, q), pl.ds(j * LANES, LANES)
+        return pltpu.make_async_remote_copy(
+            sigma.at[rows_of, at_cols], first.at[i, :, at_cols], sum_sems.at[0, i, j], sum_sems.at[1, i, j],
+            device_id=(p.s, mate), device_id_type=MESH)
+
     def products(j, carry):
         for turn in range(c):
             @pl.when(j == turn)
@@ -499,26 +511,21 @@
                 turn_in(fetch, c - 1)()
 
         deep = pl.ds(pl.multiple_of(j * ops_here * LANES, LANES), ops_here * LANES)
-        both = bdot(lp_high[...], rights[deep])
-        sigma[...] += both[:, :n] + (both[:, n:] + bdot(lp_low[...], rights[deep, pl.ds(0, n)]))
+        for i, far in ((0, 1 - side), (1, side)):
+            half = pl.ds(pl.multiple_of(far * (n // 2), 2 * SUBLANES), n // 2)
+            both = bdot(lp_high[half], rights[deep])
+            sigma[half] += both[:, :n] + (both[:, n:] + bdot(lp_low[half], rights[deep, pl.ds(0, n)]))
+
+            @pl.when(j == c - 1)
+            def _():
+                for chunk in range(c):
+                    swap_cores(i, far, chunk).start()
         return carry
 
     lax.fori_loop(0, c, products, 0)
-
-    side, core = p.o // CORES, lax.rem(p.o, CORES)
-    mate = side * CORES + 1 - core
-    facing = (1 - side) * CORES + core
-    across_mate = (1 - side) * CORES + 1 - core
-    q = p.quarter
 
     whole = polar_block
     polar = Polar(n, whole, cols, doubled, gram)
-
-    def swap_cores(i, far, j):
-        rows_of, at_cols = pl.ds((far * CORES + 1 - core) * q, q), pl.ds(j * LANES, LANES)
-        return pltpu.make_async_remote_copy(
-            sigma.at[rows_of, at_cols], first.at[i, :, at_cols], sum_sems.at[0, i, j], sum_sems.at[1, i, j],
-            device_id=(p.s, mate), device_id_type=MESH)
 
     def over(j):
         at_cols = pl.ds(j * LANES, LANES)
@@ -533,9 +540,6 @@
             source, whole.at[rows_of, at_cols], gather_sems.at[0, i, j], gather_sems.at[1, i, j],
             device_id=(p.s, target), device_id_type=MESH)
 
-    for j in range(c):
-        swap_cores(0, 1 - side, j).start()
-        swap_cores(1, side, j).start()
     for j in range(c + 1):
         if j < c:
             at_cols = pl.ds(j * LANES, LANES)

time: 138 us -> 137 us (level)
  no operation moved by 1% of the time
where the time goes in v4:
time: 137 us
  Pallas kernels  136 us (99%)
  between operations  1.45 us (1%)
    pallas_call x1, Pallas kernels, shards_planes(): pl.pallas_call(functools.partial(site_kernel, place, ops_here), out_shape...  105 us
    pallas_call x1, Pallas kernels, shards_planes(): pl.pallas_call(functools.partial(last_kernel, n, ops_here, c), out_shape=...  30.8 us

profile of v4, /device:TPU:0, one launch (start us, length us, event | category | flops | bytes accessed | tf_op | source)
XLA Modules:
  0.0 137.1 jit_solution(3830096092820315089)
XLA Ops:
  1.3 104.8 %shard_map.68 = (f32[160,640]{1,0:T(8,128)}, bf16[2560,1280]{1,0:T(8,128)(2,1)}, f32[5,640,128]{2,1,0:T(8,128)}) custom-call(f32[640,640]{1,0:T(8,128)} %bitcast.9, f32[4,640,640]{2,1,0:T(8,128)} %bitcast.7, f32[4,640,640]{2,1,0:T(8,128)} %bitcast.8, s32[1,8]{1,0:T(1,128)} %table.1, s32[1,1]{1,0:T(1,128)S(6)} %copy.7.counts), custom_call_target="tpu_custom_call" | custom-call | tf_op jit(solution)/shard_map/pallas_call | solution.py:695
  106.1 30.8 %shard_map.69 = (f32[160,640]{1,0:T(8,128)}, f32[4,640,640]{2,1,0:T(8,128)}) custom-call(f32[5,640,128]{2,1,0:T(8,128)} %get-tuple-element.7.source, bf16[2560,1280]{1,0:T(8,128)(2,1)} %get-tuple-element.8.half, f32[160,640]{1,0:T(8,128)} %get-tuple-element.9.columns), custom_call_target="tpu_custom_call" | custom-call | tf_op jit(solution)/shard_map/pallas_call | solution.py:728

commit v5 on v4

--- a/solution.py
+++ b/solution.py
@@ -450,7 +450,7 @@
         def _():
             load(right, w + 2 - ops_here).start()
 
-        at(w, [(1, line(fetch, (0, 1))), (2, line(fetch, (AHEAD, 0), (1, 1))), (2, maps.finish)])
+        at(w, [(0, line(fetch, (0, 1))), (2, line(fetch, (AHEAD, 0), (1, 1))), (2, maps.finish)])
         return carry
 
     def convert_right(w, carry):
@@ -631,8 +631,9 @@
         at = pl.ds(w * n, n)
         return pltpu.make_async_copy(half.at[at], halves_in.at[at], in_sems.at[w])
 
-    def store(w):
-        return pltpu.make_async_copy(products.at[w], rotated.at[w], out_sems.at[w])
+    def store(w, part):
+        rows_of = pl.ds(part * (n // 2), n // 2)
+        return pltpu.make_async_copy(products.at[w, rows_of], rotated.at[w, rows_of], out_sems.at[w, part])
 
     for w in range(ops_here):
         load(w).start()
@@ -660,18 +661,21 @@
 
     def rotate(w, carry):
         load(w).wait()
-        rows_of = pl.ds(pl.multiple_of(w * n, n), n)
-        both = halves_in[rows_of]
-        products[w, :, pl.ds(0, wide)] = bdot(both, double[...]) + bdot(both[:, :n], cols[:, pl.ds(0, wide)])
-        if rest:
-            ends = bdot(both, tail[...])
-            products[w, :, pl.ds(wide, rest)] = ends[:, :rest] + ends[:, rest:]
-        store(w).start()
+        for part in range(2):
+            rows_of = pl.ds(pl.multiple_of(w * n + part * (n // 2), n // 2), n // 2)
+            here = pl.ds(part * (n // 2), n // 2)
+            both = halves_in[rows_of]
+            products[w, here, pl.ds(0, wide)] = bdot(both, double[...]) + bdot(both[:, :n], cols[:, pl.ds(0, wide)])
+            if rest:
+                ends = bdot(both, tail[...])
+                products[w, here, pl.ds(wide, rest)] = ends[:, :rest] + ends[:, rest:]
+            store(w, part).start()
         return carry
 
     lax.fori_loop(0, ops_here, rotate, 0)
     for w in range(ops_here):
-        store(w).wait()
+        for part in range(2):
+            store(w, part).wait()
 
 
 def vmem():
@@ -738,7 +742,7 @@
             pltpu.VMEM((2 * n, 2 * max(n % WIDE, LANES)), BF16),
             pltpu.VMEM((ops_here, n, n), F32),
             pltpu.SemaphoreType.DMA((ops_here,)),
-            pltpu.SemaphoreType.DMA((ops_here,)),
+            pltpu.SemaphoreType.DMA((ops_here, 2)),
         ],
         compiler_params=pltpu.CompilerParams(vmem_limit_bytes=60 * 2**20),
     )(source, half, columns)

time: 137 us -> 137 us (level)
  no operation moved by 1% of the time
where the time goes in v5:
time: 137 us
  Pallas kernels  135 us (99%)
  between operations  1.45 us (1%)
    pallas_call x1, Pallas kernels, shards_planes(): pl.pallas_call(functools.partial(site_kernel, place, ops_here), out_shape...  105 us
    pallas_call x1, Pallas kernels, shards_planes(): pl.pallas_call(functools.partial(last_kernel, n, ops_here, c), out_shape=...  30.6 us

profile of v5, /device:TPU:0, one launch (start us, length us, event | category | flops | bytes accessed | tf_op | source)
XLA Modules:
  0.0 136.9 jit_solution(6365676953201222736)
XLA Ops:
  1.3 104.8 %shard_map.68 = (f32[160,640]{1,0:T(8,128)}, bf16[2560,1280]{1,0:T(8,128)(2,1)}, f32[5,640,128]{2,1,0:T(8,128)}) custom-call(f32[640,640]{1,0:T(8,128)} %bitcast.9, f32[4,640,640]{2,1,0:T(8,128)} %bitcast.7, f32[4,640,640]{2,1,0:T(8,128)} %bitcast.8, s32[1,8]{1,0:T(1,128)} %table.1, s32[1,1]{1,0:T(1,128)S(6)} %copy.7.counts), custom_call_target="tpu_custom_call" | custom-call | tf_op jit(solution)/shard_map/pallas_call | solution.py:699
  106.1 30.6 %shard_map.69 = (f32[160,640]{1,0:T(8,128)}, f32[4,640,640]{2,1,0:T(8,128)}) custom-call(f32[5,640,128]{2,1,0:T(8,128)} %get-tuple-element.7.source, bf16[2560,1280]{1,0:T(8,128)(2,1)} %get-tuple-element.8.half, f32[160,640]{1,0:T(8,128)} %get-tuple-element.9.columns), custom_call_target="tpu_custom_call" | custom-call | tf_op jit(solution)/shard_map/pallas_call | solution.py:732
